TPU v7x, 32 devices: a whole 2x2x4 slice. The times are simulated.
32 devices in a mesh: ha: 2 (over x), vert: 16 (over z, y, core).
Axes of the slice: x: 2, y: 2, z: 4, core: 2. Of those that a mesh axis runs over, the one named last changes fastest.
Arguments:
- hidden: bfloat16 [128, 16384], P('vert', 'ha'), may hold values from -6 to 6
- norm_gain: float32 [16384], P('ha'), may hold values from 0.25 to 1.75
- head_weight: bfloat16 [16384, 32064], P('ha', 'vert'), may hold values from -0.046875 to 0.046875
- targets: int32 [128], replicated, may hold values from 0 to 32063
Outputs:
- log_probs: float32 [128, 32064], P('ha', 'vert')
- target_logprob: float32 [128], P('ha')
Inputs may be any that keep to these rules, and one draw needn't show every extreme that they name: `targets`: every next token id lies in 0 to 32063.
All inputs are finite; a program needn't handle non-finite values.
Results may differ from a plain program's by a relative error of at most 0.0015.
Values may be sent and summed in bfloat16 or wider, within the bound.
A program may use at most 64 MiB of HBM per device.

v0:
```python
import jax
import jax.numpy as jnp
from jax import lax
from jax.sharding import PartitionSpec as P

D = 16384


def combined_all(part, axis, combine):
    gathered = jax.tree.map(lambda a: lax.all_gather(a, axis), part)

    def take(source):
        return jax.tree.map(lambda a: lax.dynamic_index_in_dim(a, source, 0, False), gathered)

    return lax.fori_loop(
        1, lax.axis_size(axis), lambda source, state: combine(state, take(source)), take(0)
    )


def combine(earlier, later_one):
    largest = jnp.maximum(earlier[0], later_one[0])
    expsum = earlier[1] * jnp.exp(earlier[0] - largest) + later_one[1] * jnp.exp(
        later_one[0] - largest
    )
    return (largest, expsum, earlier[2] + later_one[2])


def shards(hidden, norm_gain, head_weight, targets):
    vocab_width = head_weight.shape[1]
    vocab_start = lax.axis_index("vert") * vocab_width
    ha_count = lax.axis_size("ha")
    batch_total = hidden.shape[0] * lax.axis_size("vert")
    own_rows = batch_total // ha_count

    def partial_terms(block_rows):
        widened = block_rows.astype(jnp.float32)
        scaled = (widened * norm_gain[None, :]).astype(jnp.bfloat16)
        product = jnp.dot(scaled, head_weight, preferred_element_type=jnp.float32)
        squares = jnp.sum(widened * widened, axis=1, keepdims=True)
        return jnp.concatenate([product, squares], axis=1)

    def finish(summed, row_targets):
        unscaled = summed[:, :vocab_width]
        inverse = lax.rsqrt(summed[:, vocab_width:] / D + 1e-05)
        logits = unscaled * inverse
        local_max = jnp.max(logits, axis=1)
        local_sum = jnp.sum(jnp.exp(logits - local_max[:, None]), axis=1)
        columns = vocab_start + jnp.arange(vocab_width, dtype=jnp.int32)
        matches = row_targets[:, None] == columns[None, :]
        local_target = jnp.sum(jnp.where(matches, logits, 0.0), axis=1)
        largest, expsum, target_sum = combined_all(
            (local_max, local_sum, local_target), "vert", combine
        )
        log_total = largest + jnp.log(expsum)
        return (logits - log_total[:, None], target_sum - log_total)

    first_row = lax.axis_index("ha") * own_rows
    gathered = lax.all_gather(hidden, "vert", axis=0, tiled=True)
    summed = lax.psum_scatter(
        partial_terms(lax.slice_in_dim(gathered, 0, own_rows * lax.axis_size("ha"), axis=0)).astype(
            jnp.bfloat16
        ),
        "ha",
        scatter_dimension=0,
        tiled=True,
    ).astype(jnp.float32)
    row_targets = lax.dynamic_slice_in_dim(targets, first_row, own_rows, 0)
    log_probs, picked = finish(summed, row_targets)
    return (log_probs, picked)


def solution(mesh):
    placed = (P("vert", "ha"), P("ha"), P("ha", "vert"), P())
    return jax.shard_map(
        shards, mesh=mesh, in_specs=placed, out_specs=(P("ha", "vert"), P("ha")), check_vma=False
    )
```

profile of v0, /device:TPU:0, one launch (start us, length us, event | category | flops | bytes accessed | tf_op | source)
XLA Modules:
  0.0 159.7 jit_solution(11805804333639017836)
XLA Ops:
  7.2 0.0 all-gather.5.cloned.1.call-start
  7.2 0.7 all-gather.5.cloned.1.call-update
  7.9 0.0 reduce-scatter.4.cloned.1.call-start
  7.9 46.7 %all-gather.5.cloned.1.call-done = bf16[128,8192]{1,0:T(8,128)(2,1)} async-done(((bf16[8,8192]{1,0:T(8,128)(2,1)}), bf16[128,8192]{1,0:T(8,128)(2,1)}) %all-gather.5.cloned.1.call-update) | async-done | bytes 2097168 | tf_op jit(solution)/shard_map/all_gather | solution.py:58
  54.7 2.1 %fusion.8 = bf16[128]{0:T(256)(128)(2,1)S(1)} fusion(bf16[128,8192]{1,0:T(8,128)(2,1)} %all-gather.5.cloned.1.call-done), kind=kLoop, calls=%fused_computation.13 | loop fusion | flops 3145600 | bytes 2097408 | tf_op jit(solution)/shard_map/reduce_sum | solution.py:39
  56.8 0.0 copy-start
  56.8 0.0 copy-start.1
  56.8 14.9 %convolution_convert_fusion = bf16[128,2004]{0,1:T(8,128)(2,1)S(1)} fusion(bf16[8192,2004]{0,1:T(8,128)(2,1)} %param.8, bf16[128,8192]{1,0:T(8,128)(2,1)} %all-gather.5.cloned.1.call-done, f32[8192]{0:T(1024)} %param.7), kind=kOutput, calls=%fused_computation.14 | convolution fusion | flops 4206094848 | bytes 35476480 | tf_op jit(solution)/shard_map/dot_general | solution.py:38
  71.8 1.0 copy.8
  72.8 0.0 reduce-scatter.4.cloned.1.call-update
  72.8 0.0 copy-done
  72.9 0.1 dynamic_slice.45
  72.9 0.0 copy-done.1
  72.9 0.6 dynamic-slice
  74.2 11.8 %reduce-scatter.4.cloned.1.call-done = bf16[64,2005]{1,0:T(8,128)(2,1)} async-done(((bf16[128,2005]{1,0:T(8,128)(2,1)}), bf16[64,2005]{1,0:T(8,128)(2,1)}) %reduce-scatter.4.cloned.1.call-update) | async-done | bytes 256656
  86.0 1.2 copy.9
  87.3 0.1 convert_element_type.12
  87.4 0.3 fusion.12
  87.7 1.0 select_reduce_fusion
  88.6 0.2 dynamic-update-slice
  88.9 0.2 dynamic-update-slice.2
  89.1 0.2 dynamic-update-slice.1
  89.3 60.9 %all-reduce.3 = (f32[1024]{0:T(1024)S(1)}, f32[1024]{0:T(1024)S(1)}, f32[1024]{0:T(1024)S(1)}) all-reduce(f32[1024]{0:T(1024)S(1)} %dynamic-update-slice, f32[1024]{0:T(1024)S(1)} %dynamic-update-slice.1, f32[1024]{0:T(1024)S(1)} %dynamic-update-slice.2), channel_id=2, replica_groups=mesh['ha'=2,'vert'=16] {'vert'}, use_global_device_ids=true, to_apply=%add | all-reduce | flops 3072 | bytes 24576
  150.2 0.1 reshape.12
  150.3 0.1 reshape.13
  150.3 0.1 reshape.14
  150.4 0.7 while.19
  151.1 0.5 fusion.17
  151.6 0.1 fusion.11
  151.7 1.1 copy.7
  (24 shorter events, 0.5 us)
Async XLA Ops:
  7.2 47.5 %all-gather.5.cloned.1.call-start = ((), (), s32[]{:S(2)}) async-start(), calls=%async_computation.1 | async-start | bytes 2228224 | tf_op jit(solution)/shard_map/all_gather | solution.py:58
  7.9 78.1 %reduce-scatter.4.cloned.1.call-start = ((), (), s32[]{:S(2)}) async-start(), calls=%async_computation.2 | async-start | bytes 786432
  56.8 16.1 %copy-start = (s32[128]{0:T(128)S(1)}, s32[128]{0:T(128)}, u32[]{:S(2)}) copy-start(s32[128]{0:T(128)} %param.9) | copy-start | bytes 1540
  56.8 16.2 %copy-start.1 = (u32[32]{0:T(128)S(1)}, u32[32]{0:T(128)}, u32[]{:S(2)}) copy-start(u32[32]{0:T(128)} %constant.79) | copy-start | bytes 388
Sparse Core Ops, SparseCore 0:
  10.1 44.5 all-gather.4
  73.0 13.0 reduce-scatter.3
where the time goes:
time: 160 us
  blocking collectives  60.9 us (38%)
  waiting for transfers between devices  59.3 us (37%)
  matrix products  14.9 us (9%)
  between operations  14.8 us (9%)
  local copies, waits for them, and re-layouts  5.02 us (3%)
  other arithmetic  4.48 us (3%)
    unnamed x1, blocking collectives  60.9 us
    all_gather x1, waiting for transfers between devices, shards(): gathered = lax.all_gather(hidden, 'vert', axis=0, tiled=True)  46.7 us
    dot_general x1, matrix products, partial_terms(): product = jnp.dot(scaled, head_weight, preferred_element_type=jnp.float32)  14.9 us
    unnamed x3, waiting for transfers between devices  12.5 us
    unnamed x14, local copies, waits for them, and re-layouts  4.73 us
  transfers between devices with their start and end apart: 2, of which 2 were waited for; matrix products, arithmetic and copies ran while one was open for 0% of the time, Pallas kernels for 0%

commit v1 on v0

--- a/solution.py
+++ b/solution.py
@@ -1,6 +1,10 @@
+import functools
+
 import jax
 import jax.numpy as jnp
 from jax import lax
+from jax.experimental import pallas as pl
+from jax.experimental.pallas import tpu as pltpu
 from jax.sharding import PartitionSpec as P
 
 D = 16384
@@ -69,8 +73,284 @@
     return (log_probs, picked)
 
 
+MESH = pl.DeviceIdType.MESH
+CORES = 2
+INNER = 2
+LANES = 128
+
+
+def tiles_of(width, tile):
+    return [(start, min(tile, width - start)) for start in range(0, width, tile)]
+
+
+def kernel(
+    sizes, hidden_ref, gain_ref, weight_ref, targets_ref, out_ref, picked_ref,
+    gathered, weight, total, turned, squares, stats, square_in, square_out, *rest
+):
+    outer, chunks, depth, batch, own_rows, tiles = sizes
+    count = len(tiles)
+    outgoing, incoming = rest[:count], rest[count : 2 * count]
+    (own_sem, weight_sem, z_send, z_recv, y_send, y_recv, d_send, d_recv,
+     x_send, x_recv, q_send, q_recv, s_send, s_recv) = rest[2 * count :]
+    ha = lax.axis_index("ha")
+    me = lax.axis_index("vert")
+    vert = outer * INNER * CORES
+    z, y, c = me // (INNER * CORES), (me // CORES) % INNER, me % CORES
+
+    def at(zz, yy, cc):
+        return (ha, (zz * INNER + yy) * CORES + cc)
+
+    across = (1 - ha, me)
+    beside = at(z, 1 - y, c)
+    sibling = at(z, y, 1 - c)
+
+    own_copies = [
+        pltpu.make_async_copy(
+            hidden_ref.at[:, pl.ds(k * depth, depth)], gathered.at[k, z, y, c], own_sem.at[k]
+        )
+        for k in range(chunks)
+    ]
+    for copy in own_copies:
+        copy.start()
+    weight_copies = [
+        pltpu.make_async_copy(
+            weight_ref.at[:, pl.ds(k * depth, depth)], weight.at[k], weight_sem.at[k]
+        )
+        for k in range(chunks)
+    ]
+    for copy in weight_copies:
+        copy.start()
+
+    barrier = pltpu.get_barrier_semaphore()
+    for step in range(1, vert):
+        pl.semaphore_signal(
+            barrier, inc=1, device_id=(ha, (me + step) % vert), device_id_type=MESH
+        )
+    pl.semaphore_signal(barrier, inc=1, device_id=across, device_id_type=MESH)
+    pl.semaphore_wait(barrier, vert)
+
+    def remote(src, dst, send, recv, device):
+        return pltpu.make_async_remote_copy(
+            src_ref=src, dst_ref=dst, send_sem=send, recv_sem=recv,
+            device_id=device, device_id_type=MESH,
+        )
+
+    for k in range(chunks):
+        own_copies[k].wait()
+        mine = gathered.at[k, z, y, c]
+        for step in range(1, outer):
+            remote(mine, mine, z_send.at[k], z_recv.at[k], at((z + step) % outer, y, c)).start()
+        remote(mine, mine, y_send.at[k], y_recv.at[k], beside).start()
+
+    total[...] = jnp.zeros_like(total)
+    squares[...] = jnp.zeros_like(squares)
+
+    def three(k, send, recv, device):
+        block = gathered.at[k, pl.ds(0, outer - 1), 0, 0]
+        return remote(block, block, send.at[k], recv.at[k], device)
+
+    def four(k, send, recv, device):
+        block = gathered.at[k, :, 0, 0]
+        return remote(block, block, send.at[k], recv.at[k], device)
+
+    def eight(k, send, recv, device):
+        block = gathered.at[k, :, :, 0]
+        return remote(block, block, send.at[k], recv.at[k], device)
+
+    def stage_a(k):
+        three(k, z_send, z_recv, beside).wait_recv()
+        for step in range(1, outer):
+            piece = gathered.at[k, (z + step) % outer, y, c]
+            remote(piece, piece, y_send.at[k], y_recv.at[k], beside).start()
+        column = gathered.at[k, :, y, c]
+        remote(column, column, d_send.at[k], d_recv.at[k], sibling).start()
+
+    def stage_b(k):
+        four(k, y_send, y_recv, beside).wait_recv()
+        column = gathered.at[k, :, 1 - y, c]
+        remote(column, column, d_send.at[k], d_recv.at[k], sibling).start()
+
+    def stage_c(k):
+        eight(k, d_send, d_recv, sibling).wait_recv()
+        pltpu.make_async_copy(
+            weight_ref.at[:, pl.ds(pl.multiple_of(k * depth, depth), depth)],
+            weight.at[k], weight_sem.at[k],
+        ).wait()
+        widened = gathered[k].astype(jnp.float32).reshape(batch, depth)
+        squares[...] += sum(
+            widened[:, lane : lane + LANES] * widened[:, lane : lane + LANES]
+            for lane in range(0, depth, LANES)
+        )
+        gain = gain_ref[k]
+        return (widened * gain).astype(jnp.bfloat16)
+
+    def product(k, scaled, tile):
+        start, width = tile
+        return lax.dot_general(
+            weight[k, pl.ds(start, width), :], scaled, (((1,), (1,)), ((), ())),
+            preferred_element_type=jnp.float32,
+        )
+
+    stage_a(0)
+    stage_a(1)
+    stage_b(0)
+
+    def body(k, carry):
+        @pl.when(k + 2 < chunks)
+        def _():
+            stage_a(k + 2)
+
+        stage_b(k + 1)
+        scaled = stage_c(k)
+        for tile in tiles:
+            total[pl.ds(*tile), :] += product(k, scaled, tile)
+        return carry
+
+    lax.fori_loop(0, chunks - 1, body, 0)
+
+    last = chunks - 1
+    scaled = stage_c(last)
+    kept = pl.ds(pl.multiple_of(ha * own_rows, own_rows), own_rows)
+    given = pl.ds(pl.multiple_of((1 - ha) * own_rows, own_rows), own_rows)
+    square_out[...] = squares[given, :]
+    square_copy = remote(square_out, square_in, q_send.at[0], q_recv.at[0], across)
+    square_copy.start()
+    x_copies = []
+    for j, tile in enumerate(tiles):
+        total[pl.ds(*tile), :] += product(last, scaled, tile)
+        padded = pl.ds(tile[0], TILE)
+        turned[:, padded] = jnp.transpose(total[padded, :])
+        outgoing[j][...] = turned[given, pl.ds(*tile)].astype(jnp.bfloat16)
+        copy = remote(outgoing[j], incoming[j], x_send.at[j], x_recv.at[j], across)
+        copy.start()
+        x_copies.append(copy)
+
+    square_copy.wait_recv()
+    summed = jnp.sum(squares[kept, :] + square_in[...], axis=1, keepdims=True)
+    inverse = lax.rsqrt(summed / D + 1e-05)
+    largest = None
+    for j, tile in enumerate(tiles):
+        x_copies[j].wait_recv()
+        logits = (turned[kept, pl.ds(*tile)] + incoming[j][...].astype(jnp.float32)) * inverse
+        out_ref[:, pl.ds(*tile)] = logits
+        top = jnp.max(logits, axis=1, keepdims=True)
+        largest = top if largest is None else jnp.maximum(largest, top)
+    wanted = jnp.transpose(
+        jnp.broadcast_to(targets_ref[pl.ds(ha, 1), :].astype(jnp.float32), (LANES, LANES))
+    )[:own_rows, 0:1].astype(jnp.int32)
+    base = me * out_ref.shape[1]
+    expsum = jnp.zeros_like(largest)
+    target_sum = jnp.zeros_like(largest)
+    for start, width in tiles:
+        logits = out_ref[:, pl.ds(start, width)]
+        expsum += jnp.sum(jnp.exp(logits - largest), axis=1, keepdims=True)
+        columns = base + start + lax.broadcasted_iota(jnp.int32, logits.shape, 1)
+        target_sum += jnp.sum(
+            jnp.where(columns == wanted, logits, 0.0), axis=1, keepdims=True
+        )
+    lane = lax.broadcasted_iota(jnp.int32, (own_rows, LANES), 1)
+    packed = jnp.where(lane == 0, largest, jnp.where(lane == 1, expsum, target_sum))
+    packed = jnp.concatenate([packed] * (LANES // own_rows), axis=0)
+    stats[me] = jnp.transpose(packed)[0:8, :]
+    copies = [
+        remote(stats.at[me], stats.at[me], s_send, s_recv, (ha, (me + step) % vert))
+        for step in range(1, vert)
+    ]
+    for copy in copies:
+        copy.start()
+    others = stats.at[pl.ds(0, vert - 1)]
+    remote(others, others, s_send, s_recv, sibling).wait_recv()
+    tops = stats[:, 0, :]
+    overall = jnp.max(tops, axis=0, keepdims=True)
+    sums = jnp.sum(jnp.exp(tops - overall) * stats[:, 1, :], axis=0, keepdims=True)
+    log_total = overall + jnp.log(sums)
+    picked_ref[...] = jnp.sum(stats[:, 2, :], axis=0, keepdims=True) - log_total
+    column = jnp.transpose(jnp.broadcast_to(log_total, (LANES, LANES)))[:own_rows, 0:1]
+    for tile in tiles:
+        out_ref[:, pl.ds(*tile)] = out_ref[:, pl.ds(*tile)] - column
+
+    remote(others, others, s_send, s_recv, sibling).wait_send()
+    square_copy.wait_send()
+    for copy in x_copies:
+        copy.wait_send()
+
+    def drain(k, carry):
+        three(k, z_send, z_recv, beside).wait_send()
+        four(k, y_send, y_recv, beside).wait_send()
+        eight(k, d_send, d_recv, sibling).wait_send()
+        return carry
+
+    lax.fori_loop(0, chunks, drain, 0)
+
+
+def fused(hidden, norm_gain, head_weight, targets):
+    rows, features = hidden.shape
+    vocab_width = head_weight.shape[1]
+    vert = lax.axis_size("vert")
+    outer = vert // (INNER * CORES)
+    batch = rows * vert
+    own_rows = batch // lax.axis_size("ha")
+    chunks = CHUNKS
+    depth = features // chunks
+    tiles = tiles_of(vocab_width, TILE)
+    dma = pltpu.SemaphoreType.DMA
+    any_space = pl.BlockSpec(memory_space=pl.ANY)
+    vmem = pl.BlockSpec(memory_space=pltpu.VMEM)
+    targets = targets.reshape(2, own_rows)
+    targets = jnp.concatenate([targets] * (LANES // own_rows), axis=1)
+    log_probs, picked = pl.pallas_call(
+        functools.partial(kernel, (outer, chunks, depth, batch, own_rows, tiles)),
+        out_shape=(
+            jax.ShapeDtypeStruct((own_rows, vocab_width), jnp.float32),
+            jax.ShapeDtypeStruct((1, LANES), jnp.float32),
+        ),
+        in_specs=[any_space, vmem, any_space, vmem],
+        out_specs=(vmem, vmem),
+        scratch_shapes=[
+            pltpu.VMEM((chunks, outer, INNER, CORES, rows, depth), jnp.bfloat16),
+            pltpu.VMEM((chunks, vocab_width, depth), jnp.bfloat16),
+            pltpu.VMEM((TILE * len(tiles), batch), jnp.float32),
+            pltpu.VMEM((batch, TILE * len(tiles)), jnp.float32),
+            pltpu.VMEM((batch, LANES), jnp.float32),
+            pltpu.VMEM((vert, 8, LANES), jnp.float32),
+            pltpu.VMEM((own_rows, LANES), jnp.float32),
+            pltpu.VMEM((own_rows, LANES), jnp.float32),
+        ]
+        + [pltpu.VMEM((own_rows, width), jnp.bfloat16) for _, width in tiles] * 2
+        + [dma((chunks,))] * 8
+        + [dma((len(tiles),))] * 2
+        + [dma((1,))] * 2
+        + [dma(())] * 2,
+        compiler_params=pltpu.CompilerParams(
+            collective_id=0, has_side_effects=True, vmem_limit_bytes=60 * 1024 * 1024
+        ),
+        name="head",
+    )(hidden, norm_gain.reshape(chunks, 1, depth), head_weight.T, targets)
+    return log_probs, picked[0, :own_rows]
+
+
+def local(hidden, norm_gain, head_weight, targets):
+    rows, features = hidden.shape
+    vert, ha = lax.axis_size("vert"), lax.axis_size("ha")
+    own_rows = rows * vert // ha
+    fits = (
+        rows == 8
+        and ha == 2
+        and LANES % own_rows == 0
+        and vert % (INNER * CORES) == 0
+        and vert > INNER * CORES
+        and features % (CHUNKS * LANES) == 0
+        and head_weight.size * 2 <= 40 * 2**20
+    )
+    return (fused if fits else shards)(hidden, norm_gain, head_weight, targets)
+
+
+CHUNKS = 8
+TILE = 512
+
+
 def solution(mesh):
     placed = (P("vert", "ha"), P("ha"), P("ha", "vert"), P())
     return jax.shard_map(
-        shards, mesh=mesh, in_specs=placed, out_specs=(P("ha", "vert"), P("ha")), check_vma=False
+        local, mesh=mesh, in_specs=placed, out_specs=(P("ha", "vert"), P("ha")), check_vma=False
     )

time: 160 us -> 52.8 us (0.33)
  blocking collectives: 60.9 us -> 0 us
  waiting for transfers between devices: 59.3 us -> 0 us
  Pallas kernels: 0 us -> 47.5 us
  matrix products: 14.9 us -> 0 us
  between operations: 14.8 us -> 0.64 us
  other arithmetic: 4.48 us -> 0.64 us
    unnamed x1 -> x0, blocking collectives: 60.9 us -> none
    pallas_call x0 -> x1, Pallas kernels: none -> 47.5 us  [fused(): pl.pallas_call(functools.partial(kernel, (outer, chunks, depth, batch, ow...]
    all_gather x1 -> x0, waiting for transfers between devices: 46.7 us -> none  [shards(): gathered = lax.all_gather(hidden, 'vert', axis=0, tiled=True)]
    dot_general x1 -> x0, matrix products: 14.9 us -> none  [partial_terms(): product = jnp.dot(scaled, head_weight, preferred_element_type=jnp.float32)]
    unnamed x3 -> x0, waiting for transfers between devices: 12.5 us -> none
    reduce_sum x2 -> x0, other arithmetic: 3.05 us -> none  [the longest x1 2.08 us: partial_terms(): squares = jnp.sum(widened * widened, axis=1, keepdims=True)]
    unnamed x14 -> x1, local copies, waits for them, and re-layouts: 4.73 us -> 1.87 us
  transfers between devices with their start and end apart: 2 -> 0, of which waited for: 2 -> 0; matrix products, arithmetic and copies ran while one was open for 0% -> 0% of each run, Pallas kernels for 0% -> 0%
where the time goes in v1:
time: 52.8 us; the launch traced here: 52.5 us
  Pallas kernels  47.5 us (90%)
  local copies, waits for them, and re-layouts  3.71 us (7%)
  other arithmetic  0.64 us (1%)
  between operations  0.64 us (1%)
    pallas_call x1, Pallas kernels, fused(): pl.pallas_call(functools.partial(kernel, (outer, chunks, depth, batch, ow...  47.5 us
    unnamed x1, local copies, waits for them, and re-layouts  1.87 us
    squeeze x1, local copies, waits for them, and re-layouts, fused(): return (log_probs, picked[0, :own_rows])  1.11 us

profile of v1, /device:TPU:0, one launch (start us, length us, event | category | flops | bytes accessed | tf_op | source)
XLA Modules:
  0.0 52.5 jit_solution(4437913894680850560)
XLA Ops:
  0.6 0.7 %reshape.11 = s32[2,64]{1,0:T(2,128)S(1)} reshape(s32[128]{0:T(128)} %param.7) | data formatting | bytes 1024 | tf_op jit(solution)/shard_map/reshape | solution.py:299
  1.4 0.6 %pad_add_fusion.targets_ref = s32[2,128]{1,0:T(2,128)} fusion(s32[2,64]{1,0:T(2,128)S(1)} %reshape.11), kind=kLoop, calls=%fused_computation | loop fusion | flops 256 | bytes 1536 | tf_op jit(solution)/shard_map/concatenate | solution.py:300
  2.0 47.5 %head.1 = (f32[64,2004]{1,0:T(8,128)}, f32[1,128]{1,0:T(1,128)}) custom-call(bf16[8,8192]{1,0:T(8,128)(2,1)} %hidden_ref.1, f32[8,1,1024]{2,1,0:T(1,128)} %bitcast.5, bf16[2004,8192]{1,0:T(8,128)(2,1)} %bitcast.4, s32[2,128]{1,0:T(2,128)} %pad_add_fusion.targets_ref), custom_call_target="tpu_custom_call" | custom-call | tf_op jit(solution)/shard_map/head/pallas_call | solution.py:301
  49.5 1.1 %slice_bitcast_fusion = f32[64]{0:T(128)} fusion(f32[1,128]{1,0:T(1,128)} %get-tuple-element.5), kind=kLoop, calls=%fused_computation.1 | loop fusion | bytes 512 | tf_op jit(solution)/shard_map/squeeze | solution.py:329
  50.7 1.9 %copy.7 = f32[64,2004]{1,0:T(8,128)} copy(f32[64,2004]{1,0:T(8,128)} %get-tuple-element.8) | data formatting | bytes 1026048

commit v2 on v1

--- a/solution.py
+++ b/solution.py
@@ -77,6 +77,8 @@
 CORES = 2
 INNER = 2
 LANES = 128
+LOWEST = -3e38
+GRANT = 60 * 1024 * 1024
 
 
 def tiles_of(width, tile):
@@ -84,13 +86,13 @@
 
 
 def kernel(
-    sizes, hidden_ref, gain_ref, weight_ref, targets_ref, out_ref, picked_ref,
-    gathered, weight, total, turned, squares, stats, square_in, square_out, *rest
+    sizes, hidden_ref, gain_ref, weight_ref, targets_ref, out_ref, level_ref, picked_ref,
+    gathered, weight, total, turned, squares, stats, square_in, square_out, wanted, *rest
 ):
     outer, chunks, depth, batch, own_rows, tiles = sizes
     count = len(tiles)
     outgoing, incoming = rest[:count], rest[count : 2 * count]
-    (own_sem, weight_sem, z_send, z_recv, y_send, y_recv, d_send, d_recv,
+    (own_sem, weight_sem, f_send, z_send, z_recv, y_send, y_recv, d_send, d_recv,
      x_send, x_recv, q_send, q_recv, s_send, s_recv) = rest[2 * count :]
     ha = lax.axis_index("ha")
     me = lax.axis_index("vert")
@@ -100,6 +102,10 @@
     def at(zz, yy, cc):
         return (ha, (zz * INNER + yy) * CORES + cc)
 
+    side = z // 2
+    end, inner, far_inner = 3 * side, 1 + side, 2 - side
+    partner = end + inner - z
+    far_half = pl.ds(2 * (1 - side), 2)
     across = (1 - ha, me)
     beside = at(z, 1 - y, c)
     sibling = at(z, y, 1 - c)
@@ -118,7 +124,7 @@
         )
         for k in range(chunks)
     ]
-    for copy in weight_copies:
+    for copy in weight_copies[:AHEAD]:
         copy.start()
 
     barrier = pltpu.get_barrier_semaphore()
@@ -138,10 +144,13 @@
     for k in range(chunks):
         own_copies[k].wait()
         mine = gathered.at[k, z, y, c]
-        for step in range(1, outer):
-            remote(mine, mine, z_send.at[k], z_recv.at[k], at((z + step) % outer, y, c)).start()
+        for device in (at(far_inner, y, c), at(partner, y, c)):
+            remote(mine, mine, z_send.at[k], z_recv.at[k], device).start()
         remote(mine, mine, y_send.at[k], y_recv.at[k], beside).start()
 
+    wanted[...] = jnp.transpose(
+        jnp.broadcast_to(targets_ref[...].astype(jnp.float32), (LANES, LANES))
+    )
     total[...] = jnp.zeros_like(total)
     squares[...] = jnp.zeros_like(squares)
 
@@ -149,6 +158,10 @@
         block = gathered.at[k, pl.ds(0, outer - 1), 0, 0]
         return remote(block, block, send.at[k], recv.at[k], device)
 
+    def two(k, send, recv, device):
+        block = gathered.at[k, pl.ds(0, 2), 0, 0]
+        return remote(block, block, send.at[k], recv.at[k], device)
+
     def four(k, send, recv, device):
         block = gathered.at[k, :, 0, 0]
         return remote(block, block, send.at[k], recv.at[k], device)
@@ -157,8 +170,17 @@
         block = gathered.at[k, :, :, 0]
         return remote(block, block, send.at[k], recv.at[k], device)
 
+    def relay(k):
+        block = gathered.at[k, far_half, y, c]
+        return remote(block, block, f_send.at[k], z_recv.at[k], at(end, y, c))
+
     def stage_a(k):
         three(k, z_send, z_recv, beside).wait_recv()
+
+        @pl.when(z == inner)
+        def _():
+            relay(k).start()
+
         for step in range(1, outer):
             piece = gathered.at[k, (z + step) % outer, y, c]
             remote(piece, piece, y_send.at[k], y_recv.at[k], beside).start()
@@ -176,6 +198,15 @@
             weight_ref.at[:, pl.ds(pl.multiple_of(k * depth, depth), depth)],
             weight.at[k], weight_sem.at[k],
         ).wait()
+
+        @pl.when(k + AHEAD < chunks)
+        def _():
+            later = k + AHEAD
+            pltpu.make_async_copy(
+                weight_ref.at[:, pl.ds(pl.multiple_of(later * depth, depth), depth)],
+                weight.at[later], weight_sem.at[later],
+            ).start()
+
         widened = gathered[k].astype(jnp.float32).reshape(batch, depth)
         squares[...] += sum(
             widened[:, lane : lane + LANES] * widened[:, lane : lane + LANES]
@@ -220,7 +251,7 @@
         total[pl.ds(*tile), :] += product(last, scaled, tile)
         padded = pl.ds(tile[0], TILE)
         turned[:, padded] = jnp.transpose(total[padded, :])
-        outgoing[j][...] = turned[given, pl.ds(*tile)].astype(jnp.bfloat16)
+        outgoing[j][...] = turned[given, padded].astype(jnp.bfloat16)
         copy = remote(outgoing[j], incoming[j], x_send.at[j], x_recv.at[j], across)
         copy.start()
         x_copies.append(copy)
@@ -228,30 +259,40 @@
     square_copy.wait_recv()
     summed = jnp.sum(squares[kept, :] + square_in[...], axis=1, keepdims=True)
     inverse = lax.rsqrt(summed / D + 1e-05)
-    largest = None
-    for j, tile in enumerate(tiles):
+    vocab_width = out_ref.shape[1]
+    base = me * vocab_width
+    chosen = wanted[kept, 0:1].astype(jnp.int32) - base
+    chosen = jnp.where(chosen < vocab_width, chosen, -1)
+    lane = lax.broadcasted_iota(jnp.int32, (own_rows, LANES), 1)
+    largest = jnp.full((own_rows, LANES), LOWEST, jnp.float32)
+    expsum = jnp.zeros((own_rows, LANES), jnp.float32)
+    target_sum = jnp.zeros((own_rows, LANES), jnp.float32)
+    for j, (start, width) in enumerate(tiles):
         x_copies[j].wait_recv()
-        logits = (turned[kept, pl.ds(*tile)] + incoming[j][...].astype(jnp.float32)) * inverse
-        out_ref[:, pl.ds(*tile)] = logits
-        top = jnp.max(logits, axis=1, keepdims=True)
-        largest = top if largest is None else jnp.maximum(largest, top)
-    wanted = jnp.transpose(
-        jnp.broadcast_to(targets_ref[pl.ds(ha, 1), :].astype(jnp.float32), (LANES, LANES))
-    )[:own_rows, 0:1].astype(jnp.int32)
-    base = me * out_ref.shape[1]
-    expsum = jnp.zeros_like(largest)
-    target_sum = jnp.zeros_like(largest)
-    for start, width in tiles:
-        logits = out_ref[:, pl.ds(start, width)]
-        expsum += jnp.sum(jnp.exp(logits - largest), axis=1, keepdims=True)
-        columns = base + start + lax.broadcasted_iota(jnp.int32, logits.shape, 1)
-        target_sum += jnp.sum(
-            jnp.where(columns == wanted, logits, 0.0), axis=1, keepdims=True
-        )
-    lane = lax.broadcasted_iota(jnp.int32, (own_rows, LANES), 1)
-    packed = jnp.where(lane == 0, largest, jnp.where(lane == 1, expsum, target_sum))
+        padded = pl.ds(start, TILE)
+        logits = (turned[kept, padded] + incoming[j][...].astype(jnp.float32)) * inverse
+        out_ref[:, pl.ds(start, width)] = logits[:, :width]
+        pieces = []
+        for at_lane in range(0, width, LANES):
+            piece = logits[:, at_lane : at_lane + LANES]
+            left = width - at_lane
+            if left < LANES:
+                piece = jnp.where(lane < left, piece, LOWEST)
+            pieces.append(piece)
+            target_sum += jnp.where(lane + (start + at_lane) == chosen, piece, 0.0)
+        raised = functools.reduce(jnp.maximum, pieces, largest)
+        expsum = expsum * jnp.exp(largest - raised) + sum(
+            jnp.exp(piece - raised) for piece in pieces
+        )
+        largest = raised
+    row_max = jnp.max(largest, axis=1, keepdims=True)
+    row_sum = jnp.sum(expsum * jnp.exp(largest - row_max), axis=1, keepdims=True)
+    row_target = jnp.sum(target_sum, axis=1, keepdims=True)
+    packed = jnp.where(lane == 0, row_max, jnp.where(lane == 1, row_sum, row_target))
     packed = jnp.concatenate([packed] * (LANES // own_rows), axis=0)
-    stats[me] = jnp.transpose(packed)[0:8, :]
+    turned_stats = jnp.transpose(packed)
+    for part in range(3):
+        stats[me, :, pl.ds(part * LANES, LANES)] = turned_stats[part : part + 1, :]
     copies = [
         remote(stats.at[me], stats.at[me], s_send, s_recv, (ha, (me + step) % vert))
         for step in range(1, vert)
@@ -260,14 +301,15 @@
         copy.start()
     others = stats.at[pl.ds(0, vert - 1)]
     remote(others, others, s_send, s_recv, sibling).wait_recv()
-    tops = stats[:, 0, :]
+    tops = stats[:, 0, pl.ds(0, LANES)]
     overall = jnp.max(tops, axis=0, keepdims=True)
-    sums = jnp.sum(jnp.exp(tops - overall) * stats[:, 1, :], axis=0, keepdims=True)
+    sums = jnp.sum(
+        jnp.exp(tops - overall) * stats[:, 0, pl.ds(LANES, LANES)], axis=0, keepdims=True
+    )
     log_total = overall + jnp.log(sums)
-    picked_ref[...] = jnp.sum(stats[:, 2, :], axis=0, keepdims=True) - log_total
-    column = jnp.transpose(jnp.broadcast_to(log_total, (LANES, LANES)))[:own_rows, 0:1]
-    for tile in tiles:
-        out_ref[:, pl.ds(*tile)] = out_ref[:, pl.ds(*tile)] - column
+    picked = jnp.sum(stats[:, 0, pl.ds(2 * LANES, LANES)], axis=0, keepdims=True) - log_total
+    picked_ref[...] = picked[:, :own_rows]
+    level_ref[...] = jnp.transpose(jnp.broadcast_to(log_total, (LANES, LANES)))[:own_rows, :]
 
     remote(others, others, s_send, s_recv, sibling).wait_send()
     square_copy.wait_send()
@@ -275,12 +317,22 @@
         copy.wait_send()
 
     def drain(k, carry):
-        three(k, z_send, z_recv, beside).wait_send()
+        two(k, z_send, z_recv, beside).wait_send()
+
+        @pl.when(z == inner)
+        def _():
+            relay(k).wait_send()
+
         four(k, y_send, y_recv, beside).wait_send()
         eight(k, d_send, d_recv, sibling).wait_send()
         return carry
 
     lax.fori_loop(0, chunks, drain, 0)
+
+
+def finish(logits_ref, level_ref, picked_ref, out_ref, target_ref):
+    out_ref[...] = logits_ref[...] - level_ref[:, 0:1]
+    target_ref[...] = picked_ref[...]
 
 
 def fused(hidden, norm_gain, head_weight, targets):
@@ -294,39 +346,49 @@
     depth = features // chunks
     tiles = tiles_of(vocab_width, TILE)
     dma = pltpu.SemaphoreType.DMA
-    any_space = pl.BlockSpec(memory_space=pl.ANY)
+    hbm = pl.BlockSpec(memory_space=pltpu.HBM)
     vmem = pl.BlockSpec(memory_space=pltpu.VMEM)
-    targets = targets.reshape(2, own_rows)
-    targets = jnp.concatenate([targets] * (LANES // own_rows), axis=1)
-    log_probs, picked = pl.pallas_call(
+    logits, level, picked = pl.pallas_call(
         functools.partial(kernel, (outer, chunks, depth, batch, own_rows, tiles)),
         out_shape=(
             jax.ShapeDtypeStruct((own_rows, vocab_width), jnp.float32),
-            jax.ShapeDtypeStruct((1, LANES), jnp.float32),
+            jax.ShapeDtypeStruct((own_rows, LANES), jnp.float32),
+            jax.ShapeDtypeStruct((1, own_rows), jnp.float32),
         ),
-        in_specs=[any_space, vmem, any_space, vmem],
-        out_specs=(vmem, vmem),
+        in_specs=[hbm, vmem, hbm, vmem],
+        out_specs=(vmem, vmem, vmem),
         scratch_shapes=[
             pltpu.VMEM((chunks, outer, INNER, CORES, rows, depth), jnp.bfloat16),
             pltpu.VMEM((chunks, vocab_width, depth), jnp.bfloat16),
             pltpu.VMEM((TILE * len(tiles), batch), jnp.float32),
             pltpu.VMEM((batch, TILE * len(tiles)), jnp.float32),
             pltpu.VMEM((batch, LANES), jnp.float32),
-            pltpu.VMEM((vert, 8, LANES), jnp.float32),
+            pltpu.VMEM((vert, 1, 3 * LANES), jnp.float32),
             pltpu.VMEM((own_rows, LANES), jnp.float32),
             pltpu.VMEM((own_rows, LANES), jnp.float32),
+            pltpu.VMEM((batch, LANES), jnp.float32),
         ]
-        + [pltpu.VMEM((own_rows, width), jnp.bfloat16) for _, width in tiles] * 2
-        + [dma((chunks,))] * 8
+        + [pltpu.VMEM((own_rows, TILE), jnp.bfloat16) for _ in tiles] * 2
+        + [dma((chunks,))] * 9
         + [dma((len(tiles),))] * 2
         + [dma((1,))] * 2
         + [dma(())] * 2,
         compiler_params=pltpu.CompilerParams(
-            collective_id=0, has_side_effects=True, vmem_limit_bytes=60 * 1024 * 1024
+            collective_id=0, has_side_effects=True, vmem_limit_bytes=GRANT
         ),
         name="head",
-    )(hidden, norm_gain.reshape(chunks, 1, depth), head_weight.T, targets)
-    return log_probs, picked[0, :own_rows]
+    )(hidden, norm_gain.reshape(chunks, 1, depth), head_weight.T, targets.reshape(1, batch))
+    log_probs, target_logprob = pl.pallas_call(
+        finish,
+        out_shape=(
+            jax.ShapeDtypeStruct((own_rows, vocab_width), jnp.float32),
+            jax.ShapeDtypeStruct((1, own_rows), jnp.float32),
+        ),
+        in_specs=[vmem] * 3,
+        out_specs=(vmem, vmem),
+        name="finish",
+    )(logits, level, picked)
+    return log_probs, target_logprob.reshape(own_rows)
 
 
 def local(hidden, norm_gain, head_weight, targets):
@@ -336,16 +398,16 @@
     fits = (
         rows == 8
         and ha == 2
-        and LANES % own_rows == 0
-        and vert % (INNER * CORES) == 0
-        and vert > INNER * CORES
+        and rows * vert == LANES
+        and vert == 4 * INNER * CORES
         and features % (CHUNKS * LANES) == 0
         and head_weight.size * 2 <= 40 * 2**20
     )
     return (fused if fits else shards)(hidden, norm_gain, head_weight, targets)
 
 
-CHUNKS = 8
+CHUNKS = 4
+AHEAD = 2
 TILE = 512
 
 

time: 52.8 us -> 46.5 us (0.88)
  local copies, waits for them, and re-layouts: 3.71 us -> 0 us
  Pallas kernels: 47.5 us -> 45.7 us
  other arithmetic: 0.64 us -> 0 us
    pallas_call x1, Pallas kernels: 47.5 us -> 43.7 us  [fused(): pl.pallas_call(functools.partial(kernel, (outer, chunks, depth, batch, ow...]
    pallas_call x0 -> x1, Pallas kernels: none -> 1.96 us  [fused(): pl.pallas_call(finish, out_shape=(jax.ShapeDtypeStruct((own_rows, vocab_w...]
    unnamed x1 -> x0, local copies, waits for them, and re-layouts: 1.87 us -> none
    squeeze x1 -> x0, local copies, waits for them, and re-layouts: 1.11 us -> none  [fused(): return (log_probs, picked[0, :own_rows])]
    reshape x1 -> x0, local copies, waits for them, and re-layouts: 0.74 us -> none  [fused(): targets = targets.reshape(2, own_rows)]
    concatenate x1 -> x0, other arithmetic: 0.64 us -> none  [fused(): targets = jnp.concatenate([targets] * (LANES // own_rows), axis=1)]
where the time goes in v2:
time: 46.5 us; the launch traced here: 46.3 us
  Pallas kernels  45.7 us (98%)
  between operations  0.64 us (1%)
    pallas_call x1, Pallas kernels, fused(): pl.pallas_call(functools.partial(kernel, (outer, chunks, depth, batch, ow...  43.7 us
    pallas_call x1, Pallas kernels, fused(): pl.pallas_call(finish, out_shape=(jax.ShapeDtypeStruct((own_rows, vocab_w...  1.96 us

profile of v2, /device:TPU:0, one launch (start us, length us, event | category | flops | bytes accessed | tf_op | source)
XLA Modules:
  0.0 46.3 jit_solution(13084855895741325981)
XLA Ops:
  0.6 43.7 %head.1 = (f32[64,2004]{1,0:T(8,128)}, f32[64,128]{1,0:T(8,128)}, f32[1,64]{1,0:T(1,128)}) custom-call(bf16[8,8192]{1,0:T(8,128)(2,1)} %hidden_ref.1, f32[4,1,2048]{2,1,0:T(1,128)} %bitcast.5, bf16[2004,8192]{1,0:T(8,128)(2,1)} %bitcast.4, s32[1,128]{1,0:T(1,128)} %bitcast.6), custom_call_target="tpu_custom_call" | custom-call | tf_op jit(solution)/shard_map/head/pallas_call | solution.py:351
  44.3 2.0 %finish.1 = (f32[64,2004]{1,0:T(8,128)}, f32[1,64]{1,0:T(1,128)}) custom-call(f32[64,2004]{1,0:T(8,128)} %get-tuple-element.7.logits_ref, f32[64,128]{1,0:T(8,128)} %get-tuple-element.8.level_ref, f32[1,64]{1,0:T(1,128)} %get-tuple-element.9.picked_ref), custom_call_target="tpu_custom_call" | custom-call | tf_op jit(solution)/shard_map/finish/pallas_call | solution.py:381
